TPU v7x, 32 devices: a whole 2x2x4 slice. The times are simulated.
32 devices in a mesh: slab: 8 (over z, y), energy: 4 (over x, core).
Axes of the slice: x: 2, y: 2, z: 4, core: 2. Of those that a mesh axis runs over, the one named last changes fastest.
Arguments:
- green: bfloat16 [4, 8, 3, 2, 384, 384], P('energy', 'slab'), may hold values from -0.3125 to 0.3125
- sigma: bfloat16 [4, 8, 3, 2, 384, 384], P('energy', 'slab'), may hold values from -4 to 4
- phonon: bfloat16 [4, 8, 2, 384, 384], P('energy', 'slab'), may hold values from -4 to 4
- pair_off: int32 [8, 3], replicated, may hold values from -2 to 2, as said below
- pair_count: int32 [8], replicated, may hold values from 1 to 3, as said below
- pair_range: int32 [8, 3], replicated, may hold values from 96 to 384, as said below
Outputs:
- lesser: float32 [4, 8, 2, 384, 384], P('energy', 'slab')
Inputs may be any that keep to these rules, and one draw needn't show every extreme that they name: The partner slab k + pair_off[k, q] lies inside the grid. `pair_count`: some slab has 3 live slots. `pair_range`: a multiple of 96; some pair couples all 384 orbitals.
All inputs are finite; a program needn't handle non-finite values.
Results may differ from a plain program's by a relative error of at most 0.0035.
Values may be sent and summed in bfloat16 or wider, within the bound.
A program may use at most 64 MiB of HBM per device.

v0:
```python
import jax
import jax.numpy as jnp
from jax import lax
from jax.sharding import PartitionSpec as P


def from_behind(value, axis, steps):
    count = lax.axis_size(axis)
    leading, last = (max(0, -steps), min(count, count - steps))
    return lax.ppermute(value, axis, [(source, source + steps) for source in range(leading, last)])


def extended_2(block, sides, width):
    for axis, dim in sides:
        count = lax.axis_size(axis)
        forward = [(i, i + 1) for i in range(count - 1)]
        backward = [(target, source) for source, target in forward]
        low = lax.ppermute(
            lax.slice_in_dim(block, block.shape[dim] - width, None, axis=dim), axis, forward
        )
        high = lax.ppermute(lax.slice_in_dim(block, 0, width, axis=dim), axis, backward)
        block = jnp.concatenate([low, block, high], axis=dim)
    return block


def conj_sum(source, chosen):
    layout = (((0, 2), (0, 2)), ((), ()))

    def pair_dot(left, right):
        return lax.dot_general(left, right, layout, preferred_element_type=jnp.float32)

    real = pair_dot(source[:, 0], chosen[:, 0]) + pair_dot(source[:, 1], chosen[:, 1])
    imag = pair_dot(source[:, 1], chosen[:, 0]) - pair_dot(source[:, 0], chosen[:, 1])
    return (real, imag)


def complex_times(left, real, imag):
    first = jnp.dot(left[0], real, preferred_element_type=jnp.float32) - jnp.dot(
        left[1], imag, preferred_element_type=jnp.float32
    )
    second = jnp.dot(left[0], imag, preferred_element_type=jnp.float32) + jnp.dot(
        left[1], real, preferred_element_type=jnp.float32
    )
    return jnp.stack([first, second])


def slab_term(green_row, source, other, row_slab, diag_at, pair_off, pair_count):
    slab_total = pair_off.shape[0]
    slots = pair_off.shape[1]
    clipped = jnp.clip(other, 0, slab_total - 1)
    offsets = lax.dynamic_index_in_dim(pair_off, clipped, 0, keepdims=False)
    count = lax.dynamic_index_in_dim(pair_count, clipped, 0, keepdims=False)
    place = clipped + offsets - row_slab + 1
    slot_ids = jnp.arange(slots, dtype=jnp.int32)
    usable = (place >= 0) & (place <= 2) & (slot_ids < count)
    pick = jnp.concatenate([jnp.clip(place, 0, 2), jnp.full((1,), diag_at, jnp.int32)])
    keep = jnp.concatenate([usable, jnp.ones((1,), bool)]).astype(jnp.bfloat16)
    chosen = jnp.take(green_row, pick, axis=0) * keep[:, None, None, None]
    real, imag = conj_sum(source, chosen)
    return complex_times(green_row[diag_at], real.astype(jnp.bfloat16), imag.astype(jnp.bfloat16))


def body(green, sigma, phonon, pair_off, pair_count, pair_range):
    slab_count = green.shape[1]
    width = green.shape[-1]
    first_slab = lax.axis_index("slab") * slab_count
    sides = [from_behind(phonon, "energy", shift_by) for shift_by in (1, -1)]
    phonon_mix = (0.5 * (sides[0].astype(jnp.float32) + sides[1].astype(jnp.float32))).astype(
        jnp.bfloat16
    )
    local_range = lax.dynamic_slice_in_dim(pair_range, first_slab, slab_count, 0)
    positions = jnp.arange(width, dtype=jnp.int32)
    inside = positions[None, None, :] < local_range[:, :, None]
    square = inside[:, :, :, None] & inside[:, :, None, :]
    masked = jnp.where(square[:, :, None], sigma[0], jnp.zeros((), jnp.bfloat16))
    stacked = jnp.concatenate([masked, phonon_mix[0][:, None]], axis=1)
    extended = extended_2(stacked, (("slab", 0),), 1)
    row_slab = first_slab + 0
    green_row = green[0, 0]
    running = jnp.zeros((2, width, width), jnp.float32)
    for delta in (-1, 0, 1):
        running = running + slab_term(
            green_row,
            extended[1 + delta],
            row_slab + delta,
            row_slab,
            delta + 1,
            pair_off,
            pair_count,
        )
    results = [running]
    return jnp.stack(results)[None]


def solution(mesh):
    in_specs = (
        P("energy", "slab", None, None, None, None),
        P("energy", "slab", None, None, None, None),
        P("energy", "slab", None, None, None),
        P(),
        P(),
        P(),
    )
    out_specs = P("energy", "slab", None, None, None)
    return jax.shard_map(body, mesh=mesh, in_specs=in_specs, out_specs=out_specs, check_vma=False)
```

profile of v0, /device:TPU:10, one launch (start us, length us, event | category | flops | bytes accessed | tf_op | source)
XLA Modules:
  0.0 155.1 jit_solution(4242238613764498699)
XLA Ops:
  0.0 2.0 %collective-permute-start = (bf16[1,1,2,384,384]{4,3,1,2,0:T(8,128)(2,1)}, bf16[1,1,2,384,384]{4,3,1,2,0:T(8,128)(2,1)}, u32[]{:S(2)}, u32[]{:S(2)}) collective-permute-start(bf16[1,1,2,384,384]{4,3,1,2,0:T(8,128)(2,1)} %bitcast.181), channel_id=1, source_target_pairs={{0,1},{1,2},{2,3},{4,5},{5,6},{6,7},{8,9},{9,10},{10,11},{12,13},{... | collective-permute-start | bytes 1769480 | tf_op jit(solution)/shard_map/ppermute | solution.py:10
  2.1 3.6 %collective-permute-start.1 = (bf16[1,1,2,384,384]{4,3,1,2,0:T(8,128)(2,1)}, bf16[1,1,2,384,384]{4,3,1,2,0:T(8,128)(2,1)}, u32[]{:S(2)}, u32[]{:S(2)}) collective-permute-start(bf16[1,1,2,384,384]{4,3,1,2,0:T(8,128)(2,1)} %bitcast.182), channel_id=1, source_target_pairs={{1,0},{2,1},{3,2},{5,4},{6,5},{7,6},{9,8},{10,9},{11,10},{13,12},{... | collective-permute-start | bytes 1769480 | tf_op jit(solution)/shard_map/ppermute | solution.py:10
  5.7 1.5 and_reduce_fusion
  8.2 1.4 fusion.56
  10.6 1.0 broadcast_and_fusion
  11.8 1.7 %compare_and_fusion.3 = (pred[3]{0:T(512)(128)(4,1)S(1)}, pred[3]{0:T(512)(128)(4,1)}) fusion(pred[3]{0:T(512)(128)(4,1)S(1)} %get-tuple-element.6, s32[]{:T(128)} %bitcast.38, pred[3]{0:T(512)(128)(4,1)S(1)} %get-tuple-element.7, s32[]{:T(128)} %bitcast.22), kind=kLoop, calls=%fused_computation.119 | loop fusion | flops 12 | bytes 20 | tf_op jit(solution)/shard_map/and | solution.py:55
  14.0 3.9 %gather_fusion.2 = bf16[4,2,384,384]{3,2,1,0:T(8,128)(2,1)} fusion(bf16[3,2,384,384]{3,2,1,0:T(8,128)(2,1)} %bitcast.174, s32[1024]{0:T(1024)S(1)} %pad_clamp_fusion), kind=kCustom, calls=%fused_computation.2.clone | custom fusion | bytes 4718608 | tf_op jit(solution)/shard_map/jit(_take)/gather | solution.py:58
  17.9 1.5 bitcast_select_fusion
  19.7 1.8 %fusion = bf16[4,2,384,384]{3,2,0,1:T(8,128)(2,1)} fusion(bf16[4,2,384,384]{3,2,1,0:T(8,128)(2,1)S(1)} %copy-done.2, pred[4]{0:T(512)(128)(4,1)S(1)} %copy-done.7, bf16[4]{0:T(256)(128)(2,1)S(1)} %copy-done.8), kind=kLoop, calls=%fused_computation.5 | loop fusion | flops 2359296 | bytes 4718604 | tf_op jit(solution)/shard_map/mul | solution.py:58
  22.1 2.3 %gather_fusion.1 = bf16[4,2,384,384]{3,2,1,0:T(8,128)(2,1)} fusion(bf16[3,2,384,384]{3,2,1,0:T(8,128)(2,1)S(1)} %bitcast.175, s32[1024]{0:T(1024)S(1)} %pad_clamp_fusion.1), kind=kCustom, calls=%fused_computation.1.clone | custom fusion | bytes 4718608 | tf_op jit(solution)/shard_map/jit(_take)/gather | solution.py:58
  24.5 1.3 compare_and_fusion.5
  25.8 3.5 %fusion.1 = bf16[4,2,384,384]{3,2,0,1:T(8,128)(2,1)} fusion(bf16[4,2,384,384]{3,2,1,0:T(8,128)(2,1)} %gather_fusion.1, pred[4]{0:T(512)(128)(4,1)} %get-tuple-element.23, bf16[4]{0:T(256)(128)(2,1)} %fusion.53), kind=kLoop, calls=%fused_computation.7 | loop fusion | flops 2359296 | bytes 4718604 | tf_op jit(solution)/shard_map/mul | solution.py:58
  29.2 1.4 multiply_convert_fusion
  30.7 2.6 %fusion.55 = (bf16[4,2,384,384]{3,2,0,1:T(8,128)(2,1)}, bf16[1,4,2,384,384]{4,3,1,2,0:T(8,128)(2,1)}) fusion(bf16[1,1,2,384,384]{4,3,1,2,0:T(8,128)(2,1)S(1)} %multiply_convert_fusion, bf16[1,3,2,384,384]{4,3,1,2,0:T(8,128)(2,1)S(1)} %bitcast_select_fusion), kind=kLoop, calls=%fused_computation.122 | loop fusion | flops 1179648 | bytes 7077888 | tf_op jit(solution)/shard_map/squeeze | solution.py:84
  33.3 3.3 %collective-permute-start.3 = (bf16[1,4,2,384,384]{4,3,1,2,0:T(8,128)(2,1)}, bf16[1,4,2,384,384]{4,3,1,2,0:T(8,128)(2,1)}, u32[]{:S(2)}, u32[]{:S(2)}) collective-permute-start(bf16[1,4,2,384,384]{4,3,1,2,0:T(8,128)(2,1)} %get-tuple-element.19), channel_id=1, source_target_pairs={{4,0},{8,4},{12,8},{16,12},{20,16},{24,20},{28,24},{5,1},{9,5},{13... | collective-permute-start | bytes 7077896 | tf_op jit(solution)/shard_map/ppermute | solution.py:21
  36.7 2.4 %gather_fusion = bf16[4,2,384,384]{3,2,1,0:T(8,128)(2,1)} fusion(bf16[3,2,384,384]{3,2,1,0:T(8,128)(2,1)S(1)} %bitcast.176, s32[1024]{0:T(1024)S(1)} %pad_clamp_fusion.2), kind=kCustom, calls=%fused_computation.clone | custom fusion | bytes 4718608 | tf_op jit(solution)/shard_map/jit(_take)/gather | solution.py:58
  39.1 2.2 %fusion.2 = bf16[4,2,384,384]{3,2,0,1:T(8,128)(2,1)S(1)} fusion(bf16[4,2,384,384]{3,2,1,0:T(8,128)(2,1)} %gather_fusion, pred[4]{0:T(512)(128)(4,1)S(1)} %get-tuple-element.16, bf16[4]{0:T(256)(128)(2,1)S(1)} %fusion.52), kind=kLoop, calls=%fused_computation.9 | loop fusion | flops 2359296 | bytes 4718604 | tf_op jit(solution)/shard_map/mul | solution.py:58
  41.3 2.7 %collective-permute-start.2 = (bf16[1,4,2,384,384]{4,3,1,2,0:T(8,128)(2,1)}, bf16[1,4,2,384,384]{4,3,1,2,0:T(8,128)(2,1)S(1)}, u32[]{:S(2)}, u32[]{:S(2)}) collective-permute-start(bf16[1,4,2,384,384]{4,3,1,2,0:T(8,128)(2,1)} %get-tuple-element.19), channel_id=1, source_target_pairs={{0,4},{4,8},{8,12},{12,16},{16,20},{20,24},{24,28},{1,5},{5,9},{9,... | collective-permute-start | bytes 7077896 | tf_op jit(solution)/shard_map/ppermute | solution.py:18
  48.9 89.9 %collective-permute-done.3 = bf16[1,4,2,384,384]{4,3,1,2,0:T(8,128)(2,1)} collective-permute-done((bf16[1,4,2,384,384]{4,3,1,2,0:T(8,128)(2,1)}, bf16[1,4,2,384,384]{4,3,1,2,0:T(8,128)(2,1)}, u32[]{:S(2)}, u32[]{:S(2)}) %collective-permute-start.3) | collective-permute-done | bytes 2359328 | tf_op jit(solution)/shard_map/ppermute | solution.py:21
  138.8 2.1 %convolution_bitcast_fusion.2 = f32[384,384]{1,0:T(8,128)S(1)} fusion(bf16[4,2,384,384]{3,2,0,1:T(8,128)(2,1)} %bitcast.36, bf16[4,2,384,384]{3,2,0,1:T(8,128)(2,1)S(1)} %copy-done.4), kind=kOutput, calls=%fused_computation.17 | convolution fusion | flops 452984832 | bytes 2949120 | tf_op jit(solution)/shard_map/dot_general | solution.py:30
  140.8 2.1 %convolution_bitcast_fusion = f32[384,384]{1,0:T(8,128)S(1)} fusion(bf16[4,2,384,384]{3,2,0,1:T(8,128)(2,1)} %bitcast.36, bf16[4,2,384,384]{3,2,0,1:T(8,128)(2,1)S(1)} %copy-done.4), kind=kOutput, calls=%fused_computation.15 | convolution fusion | flops 452984832 | bytes 2949120 | tf_op jit(solution)/shard_map/dot_general | solution.py:30
  144.5 2.1 %fusion.16 = bf16[384,384]{1,0:T(8,128)(2,1)S(1)} fusion(f32[384,384]{1,0:T(8,128)S(1)} %convolution_bitcast_fusion.2, bf16[4,2,384,384]{3,2,0,1:T(8,128)(2,1)} %bitcast.36, bf16[4,2,384,384]{3,2,0,1:T(8,128)(2,1)S(1)} %copy-done.4), kind=kOutput, calls=%fused_computation.42 | convolution fusion | flops 453279744 | bytes 3244032 | tf_op jit(solution)/shard_map/dot_general | solution.py:30
  147.0 2.1 %fusion.15 = bf16[384,384]{1,0:T(8,128)(2,1)S(1)} fusion(f32[384,384]{1,0:T(8,128)S(1)} %convolution_bitcast_fusion, bf16[4,2,384,384]{3,2,0,1:T(8,128)(2,1)S(1)} %copy-done.4, bf16[4,2,384,384]{3,2,0,1:T(8,128)(2,1)} %bitcast.36), kind=kOutput, calls=%fused_computation.41 | convolution fusion | flops 453279744 | bytes 3244032 | tf_op jit(solution)/shard_map/dot_general | solution.py:30
  153.7 1.4 copy.17
  (55 shorter events, 15.0 us)
Async XLA Ops:
  0.0 10.4 %copy-start = (s32[8,3]{0,1:T(4,128)S(1)}, s32[8,3]{0,1:T(4,128)}, u32[]{:S(2)}) copy-start(s32[8,3]{0,1:T(4,128)} %param.13) | copy-start | bytes 292
  0.0 29.2 %collective-permute-start = (bf16[1,1,2,384,384]{4,3,1,2,0:T(8,128)(2,1)}, bf16[1,1,2,384,384]{4,3,1,2,0:T(8,128)(2,1)}, u32[]{:S(2)}, u32[]{:S(2)}) collective-permute-start(bf16[1,1,2,384,384]{4,3,1,2,0:T(8,128)(2,1)} %bitcast.181), channel_id=1, source_target_pairs={{0,1},{1,2},{2,3},{4,5},{5,6},{6,7},{8,9},{9,10},{10,11},{12,13},{... | collective-permute-start | bytes 1769480 | tf_op jit(solution)/shard_map/ppermute | solution.py:10
  2.1 27.2 %collective-permute-start.1 = (bf16[1,1,2,384,384]{4,3,1,2,0:T(8,128)(2,1)}, bf16[1,1,2,384,384]{4,3,1,2,0:T(8,128)(2,1)}, u32[]{:S(2)}, u32[]{:S(2)}) collective-permute-start(bf16[1,1,2,384,384]{4,3,1,2,0:T(8,128)(2,1)} %bitcast.182), channel_id=1, source_target_pairs={{1,0},{2,1},{3,2},{5,4},{6,5},{7,6},{9,8},{10,9},{11,10},{13,12},{... | collective-permute-start | bytes 1769480 | tf_op jit(solution)/shard_map/ppermute | solution.py:10
  14.0 3.9 %copy-start.6 = (bf16[1,1,3,2,384,384]{5,4,3,2,1,0:T(8,128)(2,1)S(1)}, bf16[1,1,3,2,384,384]{5,4,3,2,1,0:T(8,128)(2,1)}, u32[]{:S(2)}) copy-start(bf16[1,1,3,2,384,384]{5,4,3,2,1,0:T(8,128)(2,1)} %param.9) | copy-start | bytes 5308420
  17.9 1.8 %copy-start.2 = (bf16[4,2,384,384]{3,2,1,0:T(8,128)(2,1)S(1)}, bf16[4,2,384,384]{3,2,1,0:T(8,128)(2,1)}, u32[]{:S(2)}) copy-start(bf16[4,2,384,384]{3,2,1,0:T(8,128)(2,1)} %gather_fusion.2) | copy-start | bytes 7077892
  17.9 1.8 %copy-start.7 = (pred[4]{0:T(512)(128)(4,1)S(1)}, pred[4]{0:T(512)(128)(4,1)}, u32[]{:S(2)}) copy-start(pred[4]{0:T(512)(128)(4,1)} %get-tuple-element.12) | copy-start | bytes 16
  17.9 1.8 %copy-start.8 = (bf16[4]{0:T(256)(128)(2,1)S(1)}, bf16[4]{0:T(256)(128)(2,1)}, u32[]{:S(2)}) copy-start(bf16[4]{0:T(256)(128)(2,1)} %fusion.54) | copy-start | bytes 28
  19.7 1.8 %copy-start.9 = (pred[3]{0:T(512)(128)(4,1)S(1)}, pred[3]{0:T(512)(128)(4,1)}, u32[]{:S(2)}) copy-start(pred[3]{0:T(512)(128)(4,1)} %get-tuple-element.26) | copy-start | bytes 13
  19.7 2.4 %copy-start.1 = (bf16[1,1,3,2,384,384]{5,4,3,2,1,0:T(8,128)(2,1)S(1)}, bf16[1,1,3,2,384,384]{5,4,3,2,1,0:T(8,128)(2,1)}, u32[]{:S(2)}) copy-start(bf16[1,1,3,2,384,384]{5,4,3,2,1,0:T(8,128)(2,1)} %param.8) | copy-start | bytes 5308420
  33.3 105.5 %collective-permute-start.3 = (bf16[1,4,2,384,384]{4,3,1,2,0:T(8,128)(2,1)}, bf16[1,4,2,384,384]{4,3,1,2,0:T(8,128)(2,1)}, u32[]{:S(2)}, u32[]{:S(2)}) collective-permute-start(bf16[1,4,2,384,384]{4,3,1,2,0:T(8,128)(2,1)} %get-tuple-element.19), channel_id=1, source_target_pairs={{4,0},{8,4},{12,8},{16,12},{20,16},{24,20},{28,24},{5,1},{9,5},{13... | collective-permute-start | bytes 7077896 | tf_op jit(solution)/shard_map/ppermute | solution.py:21
  39.1 4.9 %copy-start.3 = (bf16[4,2,384,384]{3,2,0,1:T(8,128)(2,1)S(1)}, bf16[4,2,384,384]{3,2,0,1:T(8,128)(2,1)}, u32[]{:S(2)}) copy-start(bf16[4,2,384,384]{3,2,0,1:T(8,128)(2,1)} %get-tuple-element.18) | copy-start | bytes 7077892
  39.1 4.9 %copy-start.5 = (bf16[4,2,384,384]{3,2,0,1:T(8,128)(2,1)S(1)}, bf16[4,2,384,384]{3,2,0,1:T(8,128)(2,1)}, u32[]{:S(2)}) copy-start(bf16[4,2,384,384]{3,2,0,1:T(8,128)(2,1)} %fusion.1) | copy-start | bytes 7077892
  41.3 101.6 %collective-permute-start.2 = (bf16[1,4,2,384,384]{4,3,1,2,0:T(8,128)(2,1)}, bf16[1,4,2,384,384]{4,3,1,2,0:T(8,128)(2,1)S(1)}, u32[]{:S(2)}, u32[]{:S(2)}) collective-permute-start(bf16[1,4,2,384,384]{4,3,1,2,0:T(8,128)(2,1)} %get-tuple-element.19), channel_id=1, source_target_pairs={{0,4},{4,8},{8,12},{12,16},{16,20},{20,24},{24,28},{1,5},{5,9},{9,... | collective-permute-start | bytes 7077896 | tf_op jit(solution)/shard_map/ppermute | solution.py:18
  48.0 90.7 %copy-start.4 = (bf16[4,2,384,384]{3,2,0,1:T(8,128)(2,1)S(1)}, bf16[4,2,384,384]{3,2,0,1:T(8,128)(2,1)}, u32[]{:S(2)}) copy-start(bf16[4,2,384,384]{3,2,0,1:T(8,128)(2,1)} %fusion) | copy-start | bytes 7077892
where the time goes:
time: 156 us; the launch traced here: 155 us
  waiting for transfers between devices  89.9 us (58%)
  other arithmetic  21.8 us (14%)
  matrix products  19.5 us (12%)
  local copies, waits for them, and re-layouts  11.9 us (8%)
  starting transfers between devices  11.7 us (8%)
    ppermute x1, waiting for transfers between devices, extended_2(): lax.ppermute(lax.slice_in_dim(block, 0, width, axis=dim), axis, backward)  89.9 us
    dot_general x12, matrix products, pair_dot(): lax.dot_general(left, right, layout, preferred_element_type=jnp.float32)  14.6 us
    gather x3, local copies, waits for them, and re-layouts, slab_term(): chosen = jnp.take(green_row, pick, axis=0) * keep[:, None, None, None]  8.61 us
    mul x3, other arithmetic, slab_term(): chosen = jnp.take(green_row, pick, axis=0) * keep[:, None, None, None]  7.47 us
    ppermute x2, starting transfers between devices, from_behind(): lax.ppermute(value, axis, [(source, source + steps) for source in range(l...  5.68 us
    and x3, other arithmetic, slab_term(): usable = (place >= 0) & (place <= 2) & (slot_ids < count)  4.52 us
    ppermute x1, starting transfers between devices, extended_2(): lax.ppermute(lax.slice_in_dim(block, 0, width, axis=dim), axis, backward)  3.3 us
  transfers between devices with their start and end apart: 4, of which 1 were waited for; matrix products, arithmetic and copies ran while one was open for 24% of the time, Pallas kernels for 0%

commit v1 on v0

v1 whole, which is shorter than its diff:
```python
import functools

import jax
import jax.numpy as jnp
from jax import lax
from jax.experimental import pallas as pl
from jax.experimental.pallas import tpu as pltpu
from jax.sharding import PartitionSpec as P

PIECES = 4


def kernel(
    slabs,
    energies,
    off_ref,
    count_ref,
    range_ref,
    green_hbm,
    sigma_hbm,
    phonon_hbm,
    out_ref,
    green_v,
    own,
    near,
    far,
    sides,
    right,
    left,
    total,
    inner,
    send_near,
    recv_near,
    send_far,
    recv_far,
    send_side,
    recv_side,
    load_sem,
):
    i = lax.axis_index("slab")
    e = lax.axis_index("energy")
    slots = sigma_hbm.shape[0]
    width = green_v.shape[-1]
    half = width // 2
    odd = lax.rem(i, 2)
    step = 1 - 2 * odd
    partner = i + step
    onward = lax.rem(i + 2 * step + slabs, slabs)
    source = lax.rem(i - 2 * step + slabs, slabs)
    up = lax.rem(e + 1, energies)
    down = lax.rem(e - 1 + energies, energies)

    def piece(ref, unit, c):
        return ref.at[unit, c // 2, pl.ds((c % 2) * half, half)]

    def near_copy(src, unit, c):
        return pltpu.make_async_remote_copy(
            src_ref=piece(src, unit, c),
            dst_ref=piece(near, unit, c),
            send_sem=send_near.at[unit, c],
            recv_sem=recv_near.at[unit, c],
            device_id={"slab": partner},
            device_id_type=pl.DeviceIdType.MESH,
        )

    def far_copy(unit, c):
        return pltpu.make_async_remote_copy(
            src_ref=piece(near, unit, c),
            dst_ref=piece(far, unit, c),
            send_sem=send_far.at[unit, c],
            recv_sem=recv_far.at[unit, c],
            device_id={"slab": onward},
            device_id_type=pl.DeviceIdType.MESH,
        )

    def side_copy(place, target):
        return pltpu.make_async_remote_copy(
            src_ref=phonon_hbm,
            dst_ref=sides.at[place],
            send_sem=send_side.at[place],
            recv_sem=recv_side.at[place],
            device_id={"energy": target},
            device_id_type=pl.DeviceIdType.MESH,
        )

    loads = [
        pltpu.make_async_copy(green_hbm, green_v, load_sem.at[0]),
        pltpu.make_async_copy(sigma_hbm, own.at[pl.ds(0, slots)], load_sem.at[1]),
    ]
    for load in loads:
        load.start()

    barrier = pltpu.get_barrier_semaphore()
    for target in (partner, onward, source):
        pl.semaphore_signal(
            barrier, inc=1, device_id={"slab": target}, device_id_type=pl.DeviceIdType.MESH
        )
    for target in (up, down):
        pl.semaphore_signal(
            barrier, inc=1, device_id={"energy": target}, device_id_type=pl.DeviceIdType.MESH
        )
    pl.semaphore_wait(barrier, 5)

    for unit in range(slots):
        for c in range(PIECES):
            near_copy(sigma_hbm, unit, c).start()
    above = side_copy(0, up)
    below = side_copy(1, down)
    above.start()
    below.start()

    loads[0].wait()
    for place in range(3):
        real = green_v[place, 0]
        imag = green_v[place, 1]
        left[place, :, :width] = real
        left[place, :, width:] = imag
        real_t = real.T
        imag_t = imag.T
        right[place, :width, :width] = real_t
        right[place, width:, :width] = imag_t
        right[place, :width, width:] = -imag_t
        right[place, width:, width:] = real_t
    loads[1].wait()

    rows = lax.broadcasted_iota(jnp.int32, (width, width), 0)
    cols = lax.broadcasted_iota(jnp.int32, (width, width), 1)
    furthest = jnp.maximum(rows, cols)
    tile = 2 * width // 3

    def add_unit(where, buffer, delta, unit):
        k = i + delta
        valid = (k >= 0) & (k < slabs)
        k = jnp.clip(k, 0, slabs - 1)
        slot = jnp.minimum(unit, slots - 1)
        mixed = unit == slots
        place = jnp.where(mixed, delta + 1, k + off_ref[slot, k] - i + 1)
        usable = valid & (mixed | ((place >= 0) & (place <= 2) & (slot < count_ref[k])))
        pick = jnp.clip(place, 0, 2)
        reach = jnp.where(mixed, width, range_ref[slot, k])
        reach = jnp.where(usable, reach, 0)
        inside = furthest < reach
        zero = jnp.zeros((), jnp.bfloat16)
        both = jnp.concatenate(
            [jnp.where(inside, buffer[unit, 0], zero), jnp.where(inside, buffer[unit, 1], zero)],
            axis=1,
        )
        for n in range(3):
            span = slice(n * tile, (n + 1) * tile)
            total[where, :, span] += jnp.dot(
                both, right[pick, :, span], preferred_element_type=jnp.float32
            )

    def finish(where, delta, first):
        mine = total[where].astype(jnp.bfloat16)
        inner[:width, :] = mine
        inner[width:, :width] = -mine[:, width:]
        inner[width:, width:] = mine[:, :width]
        place = jnp.clip(delta + 1, 0, 2)
        for part in range(2):
            value = jnp.dot(
                left[place],
                inner[:, part * width : (part + 1) * width],
                preferred_element_type=jnp.float32,
            )
            if first:
                out_ref[part] = value
            else:
                out_ref[part] += value

    def pass_on(unit, c):
        near_copy(own, unit, c).wait_recv()
        far_copy(unit, c).start()

    total[...] = jnp.zeros_like(total)
    for c in range(PIECES // 2):
        pass_on(0, c)

    def one_unit(unit, carry):
        for c in range(PIECES // 2, PIECES):
            pass_on(unit, c)

        @pl.when(unit == 1)
        def _():
            side_copy(0, up).wait_recv()
            side_copy(1, down).wait_recv()
            for part in range(2):
                low = jnp.where(e > 0, sides[0, part].astype(jnp.float32), 0.0)
                high = jnp.where(e < energies - 1, sides[1, part].astype(jnp.float32), 0.0)
                own[slots, part] = (0.5 * (low + high)).astype(jnp.bfloat16)

        add_unit(1, near, step, unit)
        add_unit(0, own, 0, unit)

        @pl.when(unit == 1)
        def _():
            for c in range(PIECES):
                near_copy(own, slots, c).start()

        @pl.when(unit < slots)
        def _():
            for c in range(PIECES // 2):
                pass_on(unit + 1, c)

        @pl.when(unit == slots)
        def _():
            finish(0, 0, True)
            finish(1, step, False)

        for c in range(PIECES):
            far_copy(unit, c).wait_recv()
        add_unit(2, far, -step, unit)
        return carry

    lax.fori_loop(0, slots + 1, one_unit, 0)
    finish(2, -step, False)

    above.wait_send()
    below.wait_send()
    for unit in range(slots + 1):
        for c in range(PIECES):
            near_copy(sigma_hbm if unit < slots else own, unit, c).wait_send()
            far_copy(unit, c).wait_send()


def body(slabs, energies, green, sigma, phonon, pair_off, pair_count, pair_range):
    width = green.shape[-1]
    slots = sigma.shape[2]
    hbm = pl.BlockSpec(memory_space=pl.ANY)
    smem = pl.BlockSpec(memory_space=pltpu.SMEM)
    units = slots + 1
    block = (2, width, width)
    result = pl.pallas_call(
        functools.partial(kernel, slabs, energies),
        out_shape=jax.ShapeDtypeStruct(block, jnp.float32),
        in_specs=[smem, smem, smem, hbm, hbm, hbm],
        out_specs=pl.BlockSpec(memory_space=pltpu.VMEM),
        scratch_shapes=[
            pltpu.VMEM((3,) + block, jnp.bfloat16),
            pltpu.VMEM((units,) + block, jnp.bfloat16),
            pltpu.VMEM((units,) + block, jnp.bfloat16),
            pltpu.VMEM((units,) + block, jnp.bfloat16),
            pltpu.VMEM((2,) + block, jnp.bfloat16),
            pltpu.VMEM((3, 2 * width, 2 * width), jnp.bfloat16),
            pltpu.VMEM((3, width, 2 * width), jnp.bfloat16),
            pltpu.VMEM((3, width, 2 * width), jnp.float32),
            pltpu.VMEM((2 * width, 2 * width), jnp.bfloat16),
            pltpu.SemaphoreType.DMA((units, PIECES)),
            pltpu.SemaphoreType.DMA((units, PIECES)),
            pltpu.SemaphoreType.DMA((units, PIECES)),
            pltpu.SemaphoreType.DMA((units, PIECES)),
            pltpu.SemaphoreType.DMA((2,)),
            pltpu.SemaphoreType.DMA((2,)),
            pltpu.SemaphoreType.DMA((2,)),
        ],
        compiler_params=pltpu.CompilerParams(collective_id=0, has_side_effects=True),
    )(pair_off.T, pair_count, pair_range.T, green[0, 0], sigma[0, 0], phonon[0, 0])
    return result[None, None]


def solution(mesh):
    in_specs = (
        P("energy", "slab", None, None, None, None),
        P("energy", "slab", None, None, None, None),
        P("energy", "slab", None, None, None),
        P(),
        P(),
        P(),
    )
    out_specs = P("energy", "slab", None, None, None)
    run = functools.partial(body, mesh.shape["slab"], mesh.shape["energy"])
    return jax.shard_map(run, mesh=mesh, in_specs=in_specs, out_specs=out_specs, check_vma=False)
```

time: 156 us -> 70.4 us (0.45)
  the two profiles are of different devices: /device:TPU:10 before, /device:TPU:0 now
where the time goes in v1:
time: 70.4 us; the launch traced here: 70.2 us
  Pallas kernels  67.8 us (96%)
  local copies, waits for them, and re-layouts  2.36 us (3%)
    pallas_call x1, Pallas kernels, body(): pl.pallas_call(functools.partial(kernel, slabs, energies), out_shape=jax....  67.8 us
    unnamed x1, local copies, waits for them, and re-layouts  2.36 us

profile of v1, /device:TPU:0, one launch (start us, length us, event | category | flops | bytes accessed | tf_op | source)
XLA Modules:
  0.0 70.2 jit_solution(382836560635125699)
XLA Ops:
  0.0 67.8 %shard_map.64 = f32[2,384,384]{2,1,0:T(8,128)} custom-call(s32[3,8]{1,0:T(4,128)} %bitcast.10, s32[8]{0:T(128)} %count_ref.1, s32[3,8]{1,0:T(4,128)} %bitcast.11, bf16[3,2,384,384]{3,2,1,0:T(8,128)(2,1)} %bitcast.7, bf16[3,2,384,384]{3,2,1,0:T(8,128)(2,1)} %bitcast.8, bf16[2,384,384]{2,1,0:T(8,128)(2,1)} %bitcast.9), custom_call_target="tpu_custom_call" | custom-call | tf_op jit(solution)/shard_map/pallas_call | solution.py:233
  67.8 2.4 %copy.8 = f32[1,1,2,384,384]{4,3,2,1,0:T(8,128)} copy(f32[1,1,2,384,384]{4,3,2,1,0:T(8,128)} %bitcast.6) | data formatting | bytes 2359296

commit v2 on v1

v2 whole, which is shorter than its diff:
```python
import functools

import jax
import jax.numpy as jnp
from jax import lax
from jax.experimental import pallas as pl
from jax.experimental.pallas import tpu as pltpu
from jax.sharding import PartitionSpec as P

STRIPS = 4
OFFSETS = (-2, -1, 1, 2)
MESH = pl.DeviceIdType.MESH


def strip_counts(off_ref, count_ref, range_ref, k, strip):
    slots = off_ref.shape[0]
    counts = []
    for offset in OFFSETS:
        most = jnp.int32(0)
        for q in range(slots):
            used = (off_ref[q, k] == offset) & (q < count_ref[k])
            most = jnp.maximum(most, jnp.where(used, (range_ref[q, k] + strip - 1) // strip, 0))
        counts.append(most)
    return counts


def choose(slabs, strip, sizes, off_ref, count_ref, range_ref, out_ref):
    def one(k, most):
        return jnp.maximum(most, sum(strip_counts(off_ref, count_ref, range_ref, k, strip)))

    most = lax.fori_loop(0, slabs, one, jnp.int32(0))
    out_ref[0] = sum(jnp.where(most > size, 1, 0) for size in sizes[:-1])


def kernel(
    slabs,
    energies,
    packed,
    off_ref,
    count_ref,
    range_ref,
    green_hbm,
    sigma_hbm,
    phonon_hbm,
    out_ref,
    green_v,
    sigma_v,
    own,
    near,
    far,
    own_mid,
    near_mid,
    far_mid,
    sides,
    right,
    left,
    whole,
    total,
    inner,
    send_near,
    recv_near,
    send_far,
    recv_far,
    send_side,
    recv_side,
    load_sem,
):
    i = lax.axis_index("slab")
    e = lax.axis_index("energy")
    slots = sigma_hbm.shape[0]
    width = green_v.shape[-1]
    strip = width // STRIPS
    step = 1 - 2 * lax.rem(i, 2)
    partner = i + step
    goes = (i + 2 * step >= 0) & (i + 2 * step < slabs)
    comes = (i - 2 * step >= 0) & (i - 2 * step < slabs)
    onward = lax.rem(i + 2 * step + slabs, slabs)
    source = lax.rem(i - 2 * step + slabs, slabs)
    up = lax.rem(e + 1, energies)
    down = lax.rem(e - 1 + energies, energies)

    def at(main, middle, j):
        return main.at[j] if j < packed else middle.at[j - packed]

    def near_copy(j):
        return pltpu.make_async_remote_copy(
            src_ref=at(own, own_mid, j),
            dst_ref=at(near, near_mid, j),
            send_sem=send_near.at[j],
            recv_sem=recv_near.at[j],
            device_id={"slab": partner},
            device_id_type=MESH,
        )

    def far_copy(j):
        return pltpu.make_async_remote_copy(
            src_ref=at(near, near_mid, j),
            dst_ref=at(far, far_mid, j),
            send_sem=send_far.at[j],
            recv_sem=recv_far.at[j],
            device_id={"slab": onward},
            device_id_type=MESH,
        )

    def side_copy(place, target):
        return pltpu.make_async_remote_copy(
            src_ref=phonon_hbm,
            dst_ref=sides.at[place],
            send_sem=send_side.at[place],
            recv_sem=recv_side.at[place],
            device_id={"energy": target},
            device_id_type=MESH,
        )

    loads = [
        pltpu.make_async_copy(sigma_hbm, sigma_v, load_sem.at[0]),
        pltpu.make_async_copy(green_hbm, green_v, load_sem.at[1]),
    ]
    for load in loads:
        load.start()

    barrier = pltpu.get_barrier_semaphore()
    for target in (partner, onward, source):
        pl.semaphore_signal(barrier, inc=1, device_id={"slab": target}, device_id_type=MESH)
    for target in (up, down):
        pl.semaphore_signal(barrier, inc=1, device_id={"energy": target}, device_id_type=MESH)

    rows = lax.broadcasted_iota(jnp.int32, (strip, width), 0)
    cols = lax.broadcasted_iota(jnp.int32, (strip, width), 1)

    def table(k):
        counts = strip_counts(off_ref, count_ref, range_ref, k, strip)
        bases = [jnp.int32(0)]
        for count in counts[:-1]:
            bases.append(bases[-1] + count)
        return counts, bases

    own_counts, own_bases = table(i)

    def merged(offset, at_row, part, value):
        furthest = jnp.maximum(rows + at_row * strip, cols)
        for q in range(slots):
            used = (off_ref[q, i] == offset) & (q < count_ref[i])
            reach = jnp.where(used, range_ref[q, i], 0)
            value += jnp.where(furthest < reach, sigma_v[q, part, at_row].astype(jnp.float32), 0.0)
        return value.astype(jnp.bfloat16)

    def pack(j):
        offset = jnp.int32(9)
        at_row = jnp.int32(0)
        for o, count, base in zip(OFFSETS, own_counts, own_bases):
            here = (j >= base) & (j < base + count)
            offset = jnp.where(here, o, offset)
            at_row = jnp.where(here, j - base, at_row)
        at_row = jnp.clip(at_row, 0, STRIPS - 1)
        for part in range(2):
            own[j, part] = merged(offset, at_row, part, jnp.zeros((strip, width), jnp.float32))

    loads[0].wait()
    for j in range(2):
        pack(j)
    pl.semaphore_wait(barrier, 5)

    @pl.when(e < energies - 1)
    def _():
        side_copy(0, up).start()

    @pl.when(e > 0)
    def _():
        side_copy(1, down).start()

    for j in range(2, packed):
        pack(j)
        near_copy(j - 2).start()

    loads[1].wait()
    for place in range(3):
        real = green_v[place, 0]
        imag = green_v[place, 1]
        left[place, :, :width] = real
        left[place, :, width:] = imag
        real_t = real.T
        imag_t = imag.T
        right[place, :width, :width] = real_t
        right[place, width:, :width] = imag_t
        right[place, :width, width:] = -imag_t
        right[place, width:, width:] = real_t
        if place == 0:
            near_copy(packed - 2).start()
            near_copy(packed - 1).start()

    tile = 2 * width // 3

    def multiply(where, place):
        for n in range(3):
            span = slice(n * tile, (n + 1) * tile)
            total[where, :, span] += jnp.dot(
                whole[...], right[place, :, span], preferred_element_type=jnp.float32
            )

    def add_packed(where, buffer, delta):
        k = jnp.clip(i + delta, 0, slabs - 1)
        counts, bases = table(k)
        for m in range(2):
            if where == 0:
                place = jnp.int32(2 * m)
            else:
                place = m + jnp.where(delta < 0, 1, 0)
            offset = place - 1 - delta
            count = jnp.int32(0)
            base = jnp.int32(0)
            for o, some, start in zip(OFFSETS, counts, bases):
                count = jnp.where(offset == o, some, count)
                base = jnp.where(offset == o, start, base)
            for s in range(STRIPS):
                inside = jnp.where(s < count, width, 0)
                j = jnp.clip(base + s, 0, packed - 1)
                for part in range(2):
                    whole[s * strip : (s + 1) * strip, part * width : (part + 1) * width] = (
                        jnp.where(cols < inside, buffer[j, part], jnp.zeros((), jnp.bfloat16))
                    )
            multiply(where, place)

    def add_middle(where, buffer, delta):
        for s in range(STRIPS):
            for part in range(2):
                whole[s * strip : (s + 1) * strip, part * width : (part + 1) * width] = buffer[
                    s, part
                ]
        multiply(where, delta + 1)

    def finish(where, delta, first):
        mine = total[where].astype(jnp.bfloat16)
        inner[:width, :] = mine
        inner[width:, :width] = -mine[:, width:]
        inner[width:, width:] = mine[:, :width]
        for part in range(2):
            value = jnp.dot(
                left[delta + 1],
                inner[:, part * width : (part + 1) * width],
                preferred_element_type=jnp.float32,
            )
            if first:
                out_ref[part] = value
            else:
                out_ref[part] += value

    def pass_on(j):
        near_copy(j).wait_recv()

        @pl.when(goes)
        def _():
            far_copy(j).start()

    def mix():
        @pl.when(e > 0)
        def _():
            side_copy(0, up).wait_recv()

        @pl.when(e == 0)
        def _():
            sides[0] = jnp.zeros(sides.shape[1:], sides.dtype)

        @pl.when(e < energies - 1)
        def _():
            side_copy(1, down).wait_recv()

        @pl.when(e == energies - 1)
        def _():
            sides[1] = jnp.zeros(sides.shape[1:], sides.dtype)

        for s in range(STRIPS):
            for part in range(2):
                mixed = 0.5 * (
                    sides[0, part, s].astype(jnp.float32) + sides[1, part, s].astype(jnp.float32)
                )
                mixed = mixed.astype(jnp.bfloat16).astype(jnp.float32)
                own_mid[s, part] = merged(0, s, part, mixed)

    total[...] = jnp.zeros_like(total)
    for j in range(packed):
        pass_on(j)
        if j == 0:
            add_packed(0, own, 0)
        if j == 2:
            mix()
        if j == 3:
            add_middle(0, own_mid, 0)
            for s in range(STRIPS):
                near_copy(packed + s).start()
        if j == 4:
            finish(0, 0, True)

    pass_on(packed)
    add_packed(1, near, step)
    for s in range(1, STRIPS - 1):
        pass_on(packed + s)

    @pl.when(comes)
    def _():
        for j in range(packed):
            far_copy(j).wait_recv()
        add_packed(2, far, -step)

    pass_on(packed + STRIPS - 1)
    add_middle(1, near_mid, step)
    finish(1, step, False)

    @pl.when(comes)
    def _():
        for s in range(STRIPS):
            far_copy(packed + s).wait_recv()
        add_middle(2, far_mid, -step)
        finish(2, -step, False)

    @pl.when(e < energies - 1)
    def _():
        side_copy(0, up).wait_send()

    @pl.when(e > 0)
    def _():
        side_copy(1, down).wait_send()

    for j in range(packed + STRIPS):
        near_copy(j).wait_send()

    @pl.when(goes)
    def _():
        for j in range(packed + STRIPS):
            far_copy(j).wait_send()


def body(slabs, energies, green, sigma, phonon, pair_off, pair_count, pair_range):
    width = green.shape[-1]
    slots = sigma.shape[2]
    strip = width // STRIPS
    hbm = pl.BlockSpec(memory_space=pl.ANY)
    smem = pl.BlockSpec(memory_space=pltpu.SMEM)
    most = STRIPS * min(slots, len(OFFSETS))
    sizes = (most // 2, 2 * most // 3, most)
    block = (2, width, width)
    cut = (2, strip, width)
    tables = (pair_off.T, pair_count, pair_range.T)

    def run(size):
        packed = sizes[size]
        moves = packed + STRIPS
        return pl.pallas_call(
            functools.partial(kernel, slabs, energies, packed),
            out_shape=jax.ShapeDtypeStruct(block, jnp.float32),
            in_specs=[smem, smem, smem, hbm, hbm, hbm],
            out_specs=pl.BlockSpec(memory_space=pltpu.VMEM),
            scratch_shapes=[
                pltpu.VMEM((3,) + block, jnp.bfloat16),
                pltpu.VMEM((slots, 2, STRIPS, strip, width), jnp.bfloat16),
                pltpu.VMEM((packed,) + cut, jnp.bfloat16),
                pltpu.VMEM((packed,) + cut, jnp.bfloat16),
                pltpu.VMEM((packed,) + cut, jnp.bfloat16),
                pltpu.VMEM((STRIPS,) + cut, jnp.bfloat16),
                pltpu.VMEM((STRIPS,) + cut, jnp.bfloat16),
                pltpu.VMEM((STRIPS,) + cut, jnp.bfloat16),
                pltpu.VMEM((2, 2, STRIPS, strip, width), jnp.bfloat16),
                pltpu.VMEM((3, 2 * width, 2 * width), jnp.bfloat16),
                pltpu.VMEM((3, width, 2 * width), jnp.bfloat16),
                pltpu.VMEM((width, 2 * width), jnp.bfloat16),
                pltpu.VMEM((3, width, 2 * width), jnp.float32),
                pltpu.VMEM((2 * width, 2 * width), jnp.bfloat16),
                pltpu.SemaphoreType.DMA((moves,)),
                pltpu.SemaphoreType.DMA((moves,)),
                pltpu.SemaphoreType.DMA((moves,)),
                pltpu.SemaphoreType.DMA((moves,)),
                pltpu.SemaphoreType.DMA((2,)),
                pltpu.SemaphoreType.DMA((2,)),
                pltpu.SemaphoreType.DMA((2,)),
            ],
            compiler_params=pltpu.CompilerParams(collective_id=size, has_side_effects=True),
        )

    which = pl.pallas_call(
        functools.partial(choose, slabs, strip, sizes),
        out_shape=jax.ShapeDtypeStruct((1,), jnp.int32),
        in_specs=[smem, smem, smem],
        out_specs=smem,
    )(*tables)
    result = lax.switch(
        which[0],
        [run(size) for size in range(len(sizes))],
        *tables,
        green[0, 0],
        sigma[0, 0].reshape(slots, 2, STRIPS, strip, width),
        phonon[0, 0].reshape(2, STRIPS, strip, width),
    )
    return result[None, None]


def solution(mesh):
    in_specs = (
        P("energy", "slab", None, None, None, None),
        P("energy", "slab", None, None, None, None),
        P("energy", "slab", None, None, None),
        P(),
        P(),
        P(),
    )
    out_specs = P("energy", "slab", None, None, None)
    run = functools.partial(body, mesh.shape["slab"], mesh.shape["energy"])
    return jax.shard_map(run, mesh=mesh, in_specs=in_specs, out_specs=out_specs, check_vma=False)
```

time: 70.4 us -> 67.9 us (0.964)
  the two profiles are of different devices: /device:TPU:0 before, /device:TPU:10 now
where the time goes in v2:
time: 67.9 us; the launch traced here: 67.6 us
  Pallas kernels  65.4 us (96%)
  local copies, waits for them, and re-layouts  1.02 us (2%)
    pallas_call x1, Pallas kernels, body(): lax.switch(which[0], [run(size) for size in range(len(sizes))], *tables,...  63.8 us
    pallas_call x1, Pallas kernels, body(): pl.pallas_call(functools.partial(choose, slabs, strip, sizes), out_shape=...  1.61 us

profile of v2, /device:TPU:10, one launch (start us, length us, event | category | flops | bytes accessed | tf_op | source)
XLA Modules:
  0.0 67.6 jit_solution(10150487372478764619)
XLA Ops:
  0.0 1.6 %shard_map.67 = s32[1]{0:T(128)} custom-call(s32[3,8]{1,0:T(4,128)} %bitcast.21, s32[8]{0:T(128)} %count_ref.1, s32[3,8]{1,0:T(4,128)} %bitcast.25), custom_call_target="tpu_custom_call" | custom-call | tf_op jit(solution)/shard_map/pallas_call | solution.py:379
  2.3 64.3 %conditional.1 = (f32[1,1,2,384,384]{4,3,2,1,0:T(8,128)S(1)}) conditional(s32[]{:T(128)} %bitcast.5, (s32[3,8]{1,0:T(4,128)}, s32[8]{0:T(128)}, s32[3,8]{1,0:T(4,128)}, bf16[3,2,384,384]{3,2,1,0:T(8,128)(2,1)}, bf16[3,2,4,96,384]{4,3,2,1,0:T(8,128)(2,1)}, /*index=5*/bf16[2,4,96,384]{3,2,1,0:T(8,128)(2,1)}) %tuple.36, ...), branch_computations={%region_0.0_spmd, %region_1.0_spmd, %region_2.0_spmd} | conditional | bytes 8 | solution.py:385
  2.5 63.8 %branch_2_fun.1 = f32[2,384,384]{2,1,0:T(8,128)S(1)} custom-call(s32[3,8]{1,0:T(4,128)} %get-tuple-element.58.off_ref, s32[8]{0:T(128)} %get-tuple-element.59.count_ref, s32[3,8]{1,0:T(4,128)} %get-tuple-element.60.range_ref, bf16[3,2,384,384]{3,2,1,0:T(8,128)(2,1)} %get-tuple-element.61.green_hbm, bf16[3,2,4,96,384]{4,3,2,1,0:T(8,128)(2,1)} %get-tuple-element.62.sigma_hbm, ...), custom_call_target="tpu_custom_call" | custom-call | tf_op jit(solution)/shard_map/cond/branch_2_fun/pallas_call | solution.py:385
  66.6 1.0 %copy.14 = f32[1,1,2,384,384]{4,3,2,1,0:T(8,128)} copy(f32[1,1,2,384,384]{4,3,2,1,0:T(8,128)S(1)} %get-tuple-element.64) | data formatting | bytes 2359296
